TPU v7x, 32 devices: a whole 2x2x4 slice. The times are simulated.
32 devices in a mesh: dp: 4 (over z), tensor: 8 (over y, x, core).
Axes of the slice: x: 2, y: 2, z: 4, core: 2. Of those that a mesh axis runs over, the one named last changes fastest.
Arguments:
- gradient: bfloat16 [4, 2560, 8192], P('dp', None, 'tensor'), may hold values from -6 to 6
- feedback: float32 [4, 2560, 8192], P('dp', None, 'tensor'), may hold values from -4 to 4
- q_start: float32 [8192, 32], P('tensor'), may hold values from -6 to 6
Outputs:
- p_factor: float32 [2560, 32], P('tensor')
- q_factor: float32 [8192, 32], P('tensor')
- decoded: float32 [2560, 8192], P(None, 'tensor')
- residual: float32 [4, 2560, 8192], P('dp', None, 'tensor')
All inputs are finite; a program needn't handle non-finite values.
Results may differ from a plain program's by a relative error of at most 0.0003.
Values sent between devices are 32-bit elements; how exact they have to be, the bound alone decides.
A program may use at most 64 MiB of HBM per device.

v0:
```python
import jax
import jax.numpy as jnp
from jax import lax
from jax.sharding import PartitionSpec as P


def orthonormal(p_sum, gram_matrix):
    factor_low = jnp.linalg.cholesky(gram_matrix)
    return jax.scipy.linalg.solve_triangular(factor_low, p_sum.T, lower=True).T


def local(gradient, feedback, q_start):
    high = lax.Precision.HIGHEST
    merged = gradient[0].astype(jnp.float32) + feedback[0]
    row_block = lax.psum_scatter(
        jnp.dot(merged, q_start, precision=high), "tensor", scatter_dimension=0, tiled=True
    )
    row_block = lax.psum(row_block, "dp")
    gram_matrix = lax.psum(jnp.dot(row_block.T, row_block, precision=high), "tensor")
    p_factor = orthonormal(row_block, gram_matrix)
    basis_all = lax.all_gather(p_factor, "tensor", axis=0, tiled=True)
    q_local = lax.dot_general(merged, basis_all, (((0,), (0,)), ((), ())), precision=high)
    q_factor = lax.psum(q_local, "dp") / lax.axis_size("dp")
    decoded = jnp.dot(basis_all, q_factor.T, precision=high)
    residual = merged - decoded
    return (p_factor, q_factor, decoded, residual[None])


def solution(mesh):
    in_specs = (P("dp", None, "tensor"), P("dp", None, "tensor"), P("tensor", None))
    out_specs = (P("tensor", None), P("tensor", None), P(None, "tensor"), P("dp", None, "tensor"))
    return jax.shard_map(local, mesh=mesh, in_specs=in_specs, out_specs=out_specs, check_vma=False)
```

profile of v0, /device:TPU:0, one launch (start us, length us, event | category | flops | bytes accessed | tf_op | source)
XLA Modules:
  0.0 192.3 jit_solution(12324662725646355803)
XLA Ops:
  7.2 0.0 reduce-scatter.4.cloned.1.call-start
  7.2 0.8 copy-done
  8.1 12.6 %fusion.2 = f32[2560,32]{1,0:T(8,128)} fusion(f32[1024,32]{0,1:T(8,128)S(1)} %copy-done, f32[1,2560,1024]{2,1,0:T(8,128)} %param.4, bf16[1,2560,1024]{2,1,0:T(8,128)(2,1)} %param.3), kind=kOutput, calls=%fused_computation.3 | convolution fusion | flops 1011875840 | bytes 16187392
  20.7 0.0 reduce-scatter.4.cloned.1.call-update
  20.7 0.0 all-reduce.2.cloned.1.call-start
  20.8 40.0 %reduce-scatter.4.cloned.1.call-done = f32[320,32]{1,0:T(8,128)} async-done(((f32[2560,32]{1,0:T(8,128)}), f32[320,32]{1,0:T(8,128)}) %reduce-scatter.4.cloned.1.call-update) | async-done | bytes 40976
  60.8 1.0 copy.17
  61.8 19.5 %psum.21 = f32[320,32]{0,1:T(8,128)S(1)} all-reduce(f32[320,32]{0,1:T(8,128)S(1)} %copy.17), channel_id=1, replica_groups=mesh['dp'=4,'tensor'=8] {'dp'}, use_global_device_ids=true, to_apply=%region_1.0 | all-reduce | flops 10240 | bytes 81920 | tf_op jit(solution)/shard_map/psum | solution.py:18
  81.3 0.2 fusion.9
  81.5 22.3 %psum.22 = f32[32,32]{0,1:T(8,128)S(1)} all-reduce(f32[32,32]{0,1:T(8,128)S(1)} %fusion.9), channel_id=1, replica_groups=mesh['dp'=4,'tensor'=8] {'tensor'}, use_global_device_ids=true, to_apply=%region_2.0 | all-reduce | flops 1024 | bytes 8192 | tf_op jit(solution)/shard_map/psum | solution.py:19
  103.8 0.1 copy.13
  103.9 2.9 %cholesky.16 = f32[32,32]{1,0:T(8,128)S(1)} custom-call(f32[32,32]{1,0:T(8,128)S(1)} %fusion.8), custom_call_target="Cholesky" | custom-call | tf_op jit(solution)/shard_map/jit(cholesky)/cholesky | solution.py:8
  106.8 0.6 compare_reduce_fusion
  107.5 0.7 fusion.5
  108.1 2.4 %custom-call.7 = f32[1,32,32]{1,2,0:T(8,128)S(1)} custom-call(f32[1,32,32]{2,1,0:T(8,128)S(1)} %fusion.5), custom_call_target="InvertDiagBlocksLowerTriangular" | custom-call | tf_op jit(solution)/shard_map/jit(_solve_triangular)/triangular_solve | solution.py:9
  110.6 0.3 fusion.6
  110.9 9.6 %all-gather = f32[8,320,32]{1,2,0:T(8,128)S(1)} all-gather(f32[1,320,32]{1,2,0:T(8,128)S(1)} %bitcast.32), channel_id=1, replica_groups=mesh['dp'=4,'tensor'=8] {'tensor'}, dimensions={0}, use_global_device_ids=true | all-gather | bytes 368640 | tf_op jit(solution)/shard_map/all_gather | solution.py:21
  120.4 0.2 copy.14
  120.7 0.1 reshape.21
  120.8 11.0 %fusion = f32[1024,32]{0,1:T(8,128)} fusion(f32[2560,32]{0,1:T(8,128)S(1)} %reshape.21, f32[1,2560,1024]{2,1,0:T(8,128)} %param.4, bf16[1,2560,1024]{2,1,0:T(8,128)(2,1)} %param.3), kind=kOutput, calls=%fused_computation.1 | convolution fusion | flops 1011875840 | bytes 16187392 | tf_op jit(solution)/shard_map/dot_general | solution.py:22
  131.8 32.1 %all-reduce.2.cloned.1.call-done = f32[1024,32]{0,1:T(8,128)} async-done(((f32[1024,32]{0,1:T(8,128)}), f32[1024,32]{0,1:T(8,128)}) %all-reduce.2.cloned.1.call-update) | async-done | bytes 131088 | tf_op jit(solution)/shard_map/psum | solution.py:23
  163.9 0.9 broadcast_multiply_fusion
  164.8 8.5 %fusion.10 = f32[2560,1024]{1,0:T(8,128)S(1)} fusion(f32[2560,32]{0,1:T(8,128)S(1)} %reshape.21, f32[1024,32]{0,1:T(8,128)S(1)} %broadcast_multiply_fusion), kind=kOutput, calls=%fused_computation.19 | convolution fusion | flops 1006632960 | bytes 10944512 | tf_op jit(solution)/shard_map/dot_general | solution.py:24
  173.4 12.1 %fusion.4 = f32[1,2560,1024]{2,1,0:T(8,128)} fusion(f32[2560,1024]{1,0:T(8,128)S(1)} %fusion.10, f32[1,2560,1024]{2,1,0:T(8,128)} %param.4, bf16[1,2560,1024]{2,1,0:T(8,128)(2,1)S(1)} %bitcast.31), kind=kLoop, calls=%fused_computation.5 | loop fusion | flops 7864320 | bytes 36700160 | tf_op jit(solution)/shard_map/broadcast_in_dim | solution.py:26
  (15 shorter events, 0.1 us)
Async XLA Ops:
  7.2 0.9 copy-start
  7.2 53.6 %reduce-scatter.4.cloned.1.call-start = ((), (), s32[]{:S(2)}) async-start(), calls=%async_computation.2 | async-start | bytes 1474560
  20.7 143.1 %all-reduce.2.cloned.1.call-start = ((), (), s32[]{:S(2)}) async-start(), calls=%async_computation.1 | async-start | bytes 262144 | tf_op jit(solution)/shard_map/psum | solution.py:23
  110.9 62.5 %copy-start.3 = (f32[320,32]{0,1:T(8,128)}, f32[320,32]{0,1:T(8,128)S(1)}, u32[]{:S(2)}) copy-start(f32[320,32]{0,1:T(8,128)S(1)} %fusion.6) | copy-start | bytes 122884
  131.8 41.6 %slice-start = ((s8[5242880]{0:T(1024)(128)(4,1)}), s8[1048576]{0:T(1024)(128)(4,1)S(1)}, s32[]{:S(2)}) async-start(s8[5242880]{0:T(1024)(128)(4,1)} %bitcast.30), calls=%async_computation.3 | async-start | bytes 2097152
  164.8 20.7 %copy-start.2 = (f32[1024,32]{0,1:T(8,128)}, f32[1024,32]{0,1:T(8,128)S(1)}, u32[]{:S(2)}) copy-start(f32[1024,32]{0,1:T(8,128)S(1)} %broadcast_multiply_fusion) | copy-start | bytes 393220
  164.8 8.6 %slice-start.1 = ((s8[5242880]{0:T(1024)(128)(4,1)}), s8[4194304]{0:T(1024)(128)(4,1)S(1)}, s32[]{:S(2)}) async-start(s8[5242880]{0:T(1024)(128)(4,1)} %bitcast.30), calls=%async_computation.4 | async-start | bytes 8388608
  173.4 12.1 %copy-start.1 = (f32[2560,1024]{1,0:T(8,128)}, f32[2560,1024]{1,0:T(8,128)S(1)}, u32[]{:S(2)}) copy-start(f32[2560,1024]{1,0:T(8,128)S(1)} %fusion.10) | copy-start | bytes 31457284
Sparse Core Ops, SparseCore 0:
  20.9 39.8 reduce-scatter.3
  131.9 31.8 all-reduce.1
where the time goes:
time: 193 us; the launch traced here: 192 us
  waiting for transfers between devices  72.1 us (37%)
  blocking collectives  51.4 us (27%)
  matrix products  32.6 us (17%)
  other arithmetic  19.7 us (10%)
  between operations  14.2 us (7%)
  local copies, waits for them, and re-layouts  2.32 us (1%)
    unnamed x3, waiting for transfers between devices  40 us
    psum x1, waiting for transfers between devices, local(): q_factor = lax.psum(q_local, 'dp') / lax.axis_size('dp')  32.1 us
    psum x1, blocking collectives, local(): lax.psum(jnp.dot(row_block.T, row_block, precision=high), 'tensor')  22.3 us
    psum x1, blocking collectives, local(): row_block = lax.psum(row_block, 'dp')  19.5 us
    unnamed x1, matrix products  12.6 us
    broadcast_in_dim x1, other arithmetic, local(): return (p_factor, q_factor, decoded, residual[None])  12.1 us
    dot_general x1, matrix products, local(): lax.dot_general(merged, basis_all, (((0,), (0,)), ((), ())), precision=high)  11 us
    all_gather x1, blocking collectives, local(): basis_all = lax.all_gather(p_factor, 'tensor', axis=0, tiled=True)  9.56 us
  transfers between devices with their start and end apart: 2, of which 2 were waited for; matrix products, arithmetic and copies ran while one was open for 0% of the time, Pallas kernels for 0%

commit v1 on v0

--- a/solution.py
+++ b/solution.py
@@ -15,7 +15,11 @@
     row_block = lax.psum_scatter(
         jnp.dot(merged, q_start, precision=high), "tensor", scatter_dimension=0, tiled=True
     )
-    row_block = lax.psum(row_block, "dp")
+    row_block = row_block
+    for hop in (1, 2):
+        row_block = row_block + lax.ppermute(
+            row_block, "dp", [(dev, dev ^ hop) for dev in range(4)]
+        )
     gram_matrix = lax.psum(jnp.dot(row_block.T, row_block, precision=high), "tensor")
     p_factor = orthonormal(row_block, gram_matrix)
     basis_all = lax.all_gather(p_factor, "tensor", axis=0, tiled=True)

time: 193 us -> 185 us (0.959)
  blocking collectives: 51.4 us -> 31.9 us
  waiting for transfers between devices: 72.1 us -> 80.5 us
  starting transfers between devices: 0.08 us -> 4.1 us
    psum x1 -> x0, blocking collectives: 19.5 us -> none  [local(): row_block = lax.psum(row_block, 'dp')]
    ppermute x0 -> x2, waiting for transfers between devices: none -> 5.18 us  [local(): lax.ppermute(row_block, 'dp', [(dev, dev ^ hop) for dev in range(4)])]
    ppermute x0 -> x2, starting transfers between devices: none -> 4.02 us  [local(): lax.ppermute(row_block, 'dp', [(dev, dev ^ hop) for dev in range(4)])]
    psum x1, waiting for transfers between devices: 32.1 us -> 35.3 us  [local(): q_factor = lax.psum(q_local, 'dp') / lax.axis_size('dp')]
  transfers between devices with their start and end apart: 2 -> 4, of which waited for: 2 -> 4; matrix products, arithmetic and copies ran while one was open for 0% -> 0% of each run, Pallas kernels for 0% -> 0%
where the time goes in v1:
time: 185 us
  waiting for transfers between devices  80.5 us (44%)
  matrix products  32.6 us (18%)
  blocking collectives  31.9 us (17%)
  other arithmetic  19.7 us (11%)
  between operations  14.2 us (8%)
  starting transfers between devices  4.1 us (2%)
  local copies, waits for them, and re-layouts  2.32 us (1%)
    unnamed x3, waiting for transfers between devices  40 us
    psum x1, waiting for transfers between devices, local(): q_factor = lax.psum(q_local, 'dp') / lax.axis_size('dp')  35.3 us
    psum x1, blocking collectives, local(): lax.psum(jnp.dot(row_block.T, row_block, precision=high), 'tensor')  22.3 us
    unnamed x1, matrix products  12.6 us
    broadcast_in_dim x1, other arithmetic, local(): return (p_factor, q_factor, decoded, residual[None])  12.1 us
    dot_general x1, matrix products, local(): lax.dot_general(merged, basis_all, (((0,), (0,)), ((), ())), precision=high)  11 us
    all_gather x1, blocking collectives, local(): basis_all = lax.all_gather(p_factor, 'tensor', axis=0, tiled=True)  9.56 us
    dot_general x1, matrix products, local(): decoded = jnp.dot(basis_all, q_factor.T, precision=high)  8.54 us
  transfers between devices with their start and end apart: 4, of which 4 were waited for; matrix products, arithmetic and copies ran while one was open for 0% of the time, Pallas kernels for 0%

profile of v1, /device:TPU:0, one launch (start us, length us, event | category | flops | bytes accessed | tf_op | source)
XLA Modules:
  0.0 185.3 jit_solution(1346196346003850608)
XLA Ops:
  7.2 0.8 copy-done
  8.1 12.6 %fusion.2 = f32[2560,32]{1,0:T(8,128)} fusion(f32[1024,32]{0,1:T(8,128)S(1)} %copy-done, f32[1,2560,1024]{2,1,0:T(8,128)} %param.4, bf16[1,2560,1024]{2,1,0:T(8,128)(2,1)} %param.3), kind=kOutput, calls=%fused_computation.3 | convolution fusion | flops 1011875840 | bytes 16187392
  20.8 40.0 %reduce-scatter.4.cloned.1.call-done = f32[320,32]{1,0:T(8,128)} async-done(((f32[2560,32]{1,0:T(8,128)}), f32[320,32]{1,0:T(8,128)}) %reduce-scatter.4.cloned.1.call-update) | async-done | bytes 40976
  60.8 1.0 copy.17
  61.8 1.5 collective-permute-start
  63.3 2.6 %collective-permute-done = f32[320,32]{0,1:T(8,128)S(1)} collective-permute-done((f32[320,32]{0,1:T(8,128)S(1)}, f32[320,32]{0,1:T(8,128)S(1)}, u32[]{:S(2)}, u32[]{:S(2)}) %collective-permute-start) | collective-permute-done | bytes 40992 | tf_op jit(solution)/shard_map/ppermute | solution.py:20
  65.9 2.5 %collective-permute-start.1 = (f32[320,32]{0,1:T(8,128)S(1)}, f32[320,32]{0,1:T(8,128)S(1)}, u32[]{:S(2)}, u32[]{:S(2)}) collective-permute-start(f32[320,32]{0,1:T(8,128)S(1)} %add.32), channel_id=1, source_target_pairs={{0,16},{8,24},{16,0},{24,8},{1,17},{9,25},{17,1},{25,9},{2,18},{10... | collective-permute-start | bytes 122888 | tf_op jit(solution)/shard_map/ppermute | solution.py:20
  68.4 2.6 %collective-permute-done.1 = f32[320,32]{0,1:T(8,128)S(1)} collective-permute-done((f32[320,32]{0,1:T(8,128)S(1)}, f32[320,32]{0,1:T(8,128)S(1)}, u32[]{:S(2)}, u32[]{:S(2)}) %collective-permute-start.1) | collective-permute-done | bytes 40992 | tf_op jit(solution)/shard_map/ppermute | solution.py:20
  71.0 0.2 fusion.9
  71.2 22.3 %psum.14 = f32[32,32]{0,1:T(8,128)S(1)} all-reduce(f32[32,32]{0,1:T(8,128)S(1)} %fusion.9), channel_id=1, replica_groups=mesh['dp'=4,'tensor'=8] {'tensor'}, use_global_device_ids=true, to_apply=%region_1.0 | all-reduce | flops 1024 | bytes 8192 | tf_op jit(solution)/shard_map/psum | solution.py:23
  93.5 0.1 copy.13
  93.6 2.9 %cholesky.16 = f32[32,32]{1,0:T(8,128)S(1)} custom-call(f32[32,32]{1,0:T(8,128)S(1)} %fusion.8), custom_call_target="Cholesky" | custom-call | tf_op jit(solution)/shard_map/jit(cholesky)/cholesky | solution.py:8
  96.5 0.6 compare_reduce_fusion
  97.2 0.7 fusion.5
  97.8 2.4 %custom-call.7 = f32[1,32,32]{1,2,0:T(8,128)S(1)} custom-call(f32[1,32,32]{2,1,0:T(8,128)S(1)} %fusion.5), custom_call_target="InvertDiagBlocksLowerTriangular" | custom-call | tf_op jit(solution)/shard_map/jit(_solve_triangular)/triangular_solve | solution.py:9
  100.3 0.3 fusion.6
  100.6 9.6 %all-gather = f32[8,320,32]{1,2,0:T(8,128)S(1)} all-gather(f32[1,320,32]{1,2,0:T(8,128)S(1)} %bitcast.32), channel_id=1, replica_groups=mesh['dp'=4,'tensor'=8] {'tensor'}, dimensions={0}, use_global_device_ids=true | all-gather | bytes 368640 | tf_op jit(solution)/shard_map/all_gather | solution.py:25
  110.1 0.2 copy.14
  110.4 0.1 reshape.21
  110.5 11.0 %fusion = f32[1024,32]{0,1:T(8,128)} fusion(f32[2560,32]{0,1:T(8,128)S(1)} %reshape.21, f32[1,2560,1024]{2,1,0:T(8,128)} %param.4, bf16[1,2560,1024]{2,1,0:T(8,128)(2,1)} %param.3), kind=kOutput, calls=%fused_computation.1 | convolution fusion | flops 1011875840 | bytes 16187392 | tf_op jit(solution)/shard_map/dot_general | solution.py:26
  121.5 35.3 %all-reduce.2.cloned.1.call-done = f32[1024,32]{0,1:T(8,128)} async-done(((f32[1024,32]{0,1:T(8,128)}), f32[1024,32]{0,1:T(8,128)}) %all-reduce.2.cloned.1.call-update) | async-done | bytes 131088 | tf_op jit(solution)/shard_map/psum | solution.py:27
  156.8 0.9 broadcast_multiply_fusion
  157.7 8.5 %fusion.10 = f32[2560,1024]{1,0:T(8,128)S(1)} fusion(f32[2560,32]{0,1:T(8,128)S(1)} %reshape.21, f32[1024,32]{0,1:T(8,128)S(1)} %broadcast_multiply_fusion), kind=kOutput, calls=%fused_computation.19 | convolution fusion | flops 1006632960 | bytes 10944512 | tf_op jit(solution)/shard_map/dot_general | solution.py:28
  166.3 12.1 %fusion.4 = f32[1,2560,1024]{2,1,0:T(8,128)} fusion(f32[2560,1024]{1,0:T(8,128)S(1)} %fusion.10, f32[1,2560,1024]{2,1,0:T(8,128)} %param.4, bf16[1,2560,1024]{2,1,0:T(8,128)(2,1)S(1)} %bitcast.31), kind=kLoop, calls=%fused_computation.5 | loop fusion | flops 7864320 | bytes 36700160 | tf_op jit(solution)/shard_map/broadcast_in_dim | solution.py:30
  (20 shorter events, 0.2 us)
Async XLA Ops:
  7.2 0.9 copy-start
  7.2 53.6 %reduce-scatter.4.cloned.1.call-start = ((), (), s32[]{:S(2)}) async-start(), calls=%async_computation.2 | async-start | bytes 1474560
  20.7 136.1 %all-reduce.2.cloned.1.call-start = ((), (), s32[]{:S(2)}) async-start(), calls=%async_computation.1 | async-start | bytes 262144 | tf_op jit(solution)/shard_map/psum | solution.py:27
  61.8 4.1 %collective-permute-start = (f32[320,32]{0,1:T(8,128)S(1)}, f32[320,32]{0,1:T(8,128)S(1)}, u32[]{:S(2)}, u32[]{:S(2)}) collective-permute-start(f32[320,32]{0,1:T(8,128)S(1)} %copy.17), channel_id=1, source_target_pairs={{0,8},{8,0},{16,24},{24,16},{1,9},{9,1},{17,25},{25,17},{2,10},{10... | collective-permute-start | bytes 122888 | tf_op jit(solution)/shard_map/ppermute | solution.py:20
  65.9 5.1 %collective-permute-start.1 = (f32[320,32]{0,1:T(8,128)S(1)}, f32[320,32]{0,1:T(8,128)S(1)}, u32[]{:S(2)}, u32[]{:S(2)}) collective-permute-start(f32[320,32]{0,1:T(8,128)S(1)} %add.32), channel_id=1, source_target_pairs={{0,16},{8,24},{16,0},{24,8},{1,17},{9,25},{17,1},{25,9},{2,18},{10... | collective-permute-start | bytes 122888 | tf_op jit(solution)/shard_map/ppermute | solution.py:20
  100.6 65.7 %copy-start.3 = (f32[320,32]{0,1:T(8,128)}, f32[320,32]{0,1:T(8,128)S(1)}, u32[]{:S(2)}) copy-start(f32[320,32]{0,1:T(8,128)S(1)} %fusion.6) | copy-start | bytes 122884
  121.5 44.8 %slice-start = ((s8[5242880]{0:T(1024)(128)(4,1)}), s8[1048576]{0:T(1024)(128)(4,1)S(1)}, s32[]{:S(2)}) async-start(s8[5242880]{0:T(1024)(128)(4,1)} %bitcast.30), calls=%async_computation.3 | async-start | bytes 2097152
  157.7 20.7 %copy-start.2 = (f32[1024,32]{0,1:T(8,128)}, f32[1024,32]{0,1:T(8,128)S(1)}, u32[]{:S(2)}) copy-start(f32[1024,32]{0,1:T(8,128)S(1)} %broadcast_multiply_fusion) | copy-start | bytes 393220
  157.7 8.6 %slice-start.1 = ((s8[5242880]{0:T(1024)(128)(4,1)}), s8[4194304]{0:T(1024)(128)(4,1)S(1)}, s32[]{:S(2)}) async-start(s8[5242880]{0:T(1024)(128)(4,1)} %bitcast.30), calls=%async_computation.4 | async-start | bytes 8388608
  166.3 12.1 %copy-start.1 = (f32[2560,1024]{1,0:T(8,128)}, f32[2560,1024]{1,0:T(8,128)S(1)}, u32[]{:S(2)}) copy-start(f32[2560,1024]{1,0:T(8,128)S(1)} %fusion.10) | copy-start | bytes 31457284
Sparse Core Ops, SparseCore 0:
  20.9 39.8 reduce-scatter.3
  121.6 35.1 all-reduce.1
